TPU v7x, 32 devices: a whole 2x2x4 slice. The times are simulated.
32 devices in a mesh: region: 8 (over z, core), feat: 4 (over y, x).
Axes of the slice: x: 2, y: 2, z: 4, core: 2. Of those that a mesh axis runs over, the one named last changes fastest.
Arguments:
- node_lat: bfloat16 [3072, 512], P(('region', 'feat')), may hold values from -6 to 6
- edge_lat: bfloat16 [24576, 512], P(('region', 'feat')), may hold values from -6 to 6
- receiver_row: int32 [24576], P('region'), may hold values from 0 to 383
- sender_slot: int32 [24576], P('region'), may hold values from 0 to 511, as said below
- send_rows: int32 [8, 8, 16], P('region'), may hold values from 0 to 383
- w_edge_in: bfloat16 [3, 512, 512], P(None, 'feat'), may hold values from -0.15625 to 0.15625
- w_edge_out: bfloat16 [512, 512], P('feat'), may hold values from -0.25 to 0.25
- w_node_in: bfloat16 [2, 512, 512], P(None, 'feat'), may hold values from -0.1875 to 0.1875
- w_node_out: bfloat16 [512, 512], P('feat'), may hold values from -0.25 to 0.25
- edge_gain: float32 [512], P('feat'), may hold values from 0.1 to 1.9
- node_gain: float32 [512], P('feat'), may hold values from 0.1 to 1.9
- node_cot: bfloat16 [3072, 512], P(('region', 'feat')), may hold values from -6 to 6
- edge_cot: bfloat16 [24576, 512], P(('region', 'feat')), may hold values from -6 to 6
Outputs:
- node_new: bfloat16 [3072, 512], P(('region', 'feat'))
- edge_new: bfloat16 [24576, 512], P(('region', 'feat'))
- node_grad: float32 [3072, 512], P(('region', 'feat'))
- edge_grad: float32 [24576, 512], P(('region', 'feat'))
- grad_edge_in: float32 [3, 512, 512], P(None, 'feat')
- grad_edge_out: float32 [512, 512], P('feat')
- grad_node_in: float32 [2, 512, 512], P(None, 'feat')
- grad_node_out: float32 [512, 512], P('feat')
Inputs may be any that keep to these rules, and one draw needn't show every extreme that they name: `receiver_row`: edge e lies in region e // 3072; its receiver is that row of the region's 384 nodes. `sender_slot`: A value below 384 is a row of the edge's own region; a value 384 + p * 16 + s names the node that region p lists in slot s for the edge's region, and p is never the edge's own region. send_rows[p, r, s] is a row of region p's 384 nodes.
All inputs are finite; a program needn't handle non-finite values.
Results may differ from a plain program's by a relative error of at most 0.02.
Values may be sent and summed in bfloat16 or wider, within the bound.
No kernel may reach another device: no remote copies, remote signals or barrier semaphores. Data moves between devices by JAX's collectives and lax.ppermute only.
A program may use at most 64 MiB of HBM per device.

v0:
```python
import jax
import jax.numpy as jnp
from jax import lax
from jax.sharding import PartitionSpec as P

EPSILON = 1e-05


def apply_swish(values):
    return values * jax.nn.sigmoid(values)


def swish_slope(values):
    sigmoid_value = jax.nn.sigmoid(values)
    return sigmoid_value * (1.0 + values * (1.0 - sigmoid_value))


def layer_norm(values, gain_values, breadth):
    sums = jnp.sum(values, axis=1)
    squares = jnp.sum(values * values, axis=1)
    average = sums[:, None] / breadth
    variance = squares[:, None] / breadth - average * average
    inverse = lax.rsqrt(variance + EPSILON)
    normed = (values - average) * inverse
    return (normed, inverse, normed * gain_values)


def layer_norm_back(cotangent, normed, inverse, gain_values, breadth):
    scaled = cotangent * gain_values
    first_sum = jnp.sum(scaled, axis=1)
    second_sum = jnp.sum(scaled * normed, axis=1)
    return (
        inverse * (scaled - first_sum[:, None] / breadth - normed * (second_sum[:, None] / breadth))
    ).astype(jnp.bfloat16)


def matmul_back(first_operand, second_operand):
    return lax.dot_general(
        first_operand, second_operand, (((1,), (1,)), ((), ())), preferred_element_type=jnp.float32
    )


def transposed(first_operand, second_operand):
    return lax.dot_general(
        first_operand, second_operand, (((0,), (0,)), ((), ())), preferred_element_type=jnp.float32
    )


def split_parts(values):
    upper_part = lax.optimization_barrier(values.astype(jnp.bfloat16))
    lower_part = (values - upper_part.astype(jnp.float32)).astype(jnp.bfloat16)
    return (upper_part, lower_part)


def shards(
    node_lat,
    edge_lat,
    receiver_row,
    sender_slot,
    send_rows,
    w_edge_in,
    w_edge_out,
    w_node_in,
    w_node_out,
    edge_gain,
    node_gain,
    node_cot,
    edge_cot,
):
    node_latent_rows = node_lat
    edge_latent_rows = edge_lat
    node_cot_rows = node_cot
    edge_cot_rows = edge_cot
    node_lat, edge_lat, node_cot, edge_cot = (
        lax.all_to_all(node_latent_rows, "feat", split_axis=1, concat_axis=0, tiled=True),
        lax.all_to_all(edge_latent_rows, "feat", split_axis=1, concat_axis=0, tiled=True),
        lax.all_to_all(node_cot_rows, "feat", split_axis=1, concat_axis=0, tiled=True),
        lax.all_to_all(edge_cot_rows, "feat", split_axis=1, concat_axis=0, tiled=True),
    )
    breadth = w_edge_out.shape[1]
    portion = w_edge_out.shape[0]
    node_count = node_lat.shape[0]
    edge_count = edge_lat.shape[0]
    feat_count = lax.axis_size("feat")
    feat_here = lax.axis_index("feat")
    offset = feat_here * portion
    stacked = jnp.concatenate([w_edge_in, w_edge_out[None], w_node_in, w_node_out[None]], axis=0)
    send_list = send_rows[0]
    outgoing = node_lat[send_list]
    incoming = lax.all_to_all(outgoing, "region", split_axis=0, concat_axis=0, tiled=True)
    lookup_table = jnp.concatenate([node_lat, incoming.reshape(-1, portion)], axis=0)
    senders = lookup_table[sender_slot]
    receivers = node_lat[receiver_row]
    node_ids = jnp.arange(node_count, dtype=jnp.int32)
    incidence = (node_ids[:, None] == receiver_row[None, :]).astype(jnp.bfloat16)
    edge_share = edge_count // feat_count
    full_weights = lax.all_gather(stacked, "feat", axis=1, tiled=True)
    full_gains = lax.all_gather(
        jnp.stack([edge_gain, node_gain], axis=0), "feat", axis=1, tiled=True
    )
    lookup_full = lax.all_gather(lookup_table, "feat", axis=1, tiled=True)
    local_receivers = lax.dynamic_slice_in_dim(receiver_row, feat_here * edge_share, edge_share)
    local_senders = lax.dynamic_slice_in_dim(sender_slot, feat_here * edge_share, edge_share)
    sender_rows = lookup_full[local_senders]
    receiver_rows = lookup_full[local_receivers]
    pre_hidden_rows = (
        jnp.dot(edge_latent_rows, full_weights[0], preferred_element_type=jnp.float32)
        + jnp.dot(sender_rows, full_weights[1], preferred_element_type=jnp.float32)
        + jnp.dot(receiver_rows, full_weights[2], preferred_element_type=jnp.float32)
    )
    hidden_rows = apply_swish(pre_hidden_rows).astype(jnp.bfloat16)
    edge_mix_rows = jnp.dot(hidden_rows, full_weights[3], preferred_element_type=jnp.float32)
    edge_normed_rows, edge_inverse_rows, edge_update_rows = layer_norm(
        edge_mix_rows, full_gains[0], breadth
    )
    edge_new_rows = (edge_latent_rows.astype(jnp.float32) + edge_update_rows).astype(jnp.bfloat16)
    row_incidence = (node_ids[:, None] == local_receivers[None, :]).astype(jnp.bfloat16)
    pooled_rows = lax.psum_scatter(
        jnp.dot(row_incidence, edge_new_rows, preferred_element_type=jnp.float32).astype(
            jnp.bfloat16
        ),
        "feat",
        scatter_dimension=0,
        tiled=True,
    )
    node_pre_rows = jnp.dot(
        node_latent_rows, full_weights[4], preferred_element_type=jnp.float32
    ) + jnp.dot(pooled_rows, full_weights[5], preferred_element_type=jnp.float32)
    node_hidden_rows = apply_swish(node_pre_rows).astype(jnp.bfloat16)
    node_mix_rows = jnp.dot(node_hidden_rows, full_weights[6], preferred_element_type=jnp.float32)
    node_normed_rows, node_inverse_rows, node_update_rows = layer_norm(
        node_mix_rows, full_gains[1], breadth
    )
    node_new_rows = (node_latent_rows.astype(jnp.float32) + node_update_rows).astype(jnp.bfloat16)
    node_mix_grad_rows = layer_norm_back(
        node_cot_rows.astype(jnp.float32),
        node_normed_rows,
        node_inverse_rows,
        full_gains[1],
        breadth,
    )
    node_pre_grad_rows = (
        matmul_back(node_mix_grad_rows, full_weights[6]) * swish_slope(node_pre_rows)
    ).astype(jnp.bfloat16)
    node_pre_wide, node_mix_wide = (
        lax.all_gather(node_pre_grad_rows, "feat", axis=0, tiled=True),
        lax.all_gather(node_mix_grad_rows, "feat", axis=0, tiled=True),
    )
    pooled_full = matmul_back(node_pre_wide, full_weights[5])
    edge_total_rows = edge_cot_rows.astype(jnp.float32) + pooled_full[local_receivers]
    edge_mix_grad_rows = layer_norm_back(
        edge_total_rows, edge_normed_rows, edge_inverse_rows, full_gains[0], breadth
    )
    pre_grad_rows = (
        matmul_back(edge_mix_grad_rows, full_weights[3]) * swish_slope(pre_hidden_rows)
    ).astype(jnp.bfloat16)
    pre_wide, edge_mix_wide = (
        lax.all_gather(pre_grad_rows, "feat", axis=0, tiled=True),
        lax.all_gather(edge_mix_grad_rows, "feat", axis=0, tiled=True),
    )
    pooled_grad = lax.dynamic_slice_in_dim(pooled_full, offset, portion, 1)
    edge_total = edge_cot.astype(jnp.float32) + pooled_grad[receiver_row]
    node_hidden, pooled, hidden = (
        lax.all_to_all(node_hidden_rows, "feat", split_axis=1, concat_axis=0, tiled=True),
        lax.all_to_all(pooled_rows, "feat", split_axis=1, concat_axis=0, tiled=True),
        lax.all_to_all(hidden_rows, "feat", split_axis=1, concat_axis=0, tiled=True),
    )
    grad_node_second_layer = transposed(node_hidden, node_mix_wide)
    node_direct = matmul_back(node_pre_wide, w_node_in[0])
    grad_node_latent = transposed(node_lat, node_pre_wide)
    grad_node_pooled = transposed(pooled, node_pre_wide)
    grad_edge_second_layer = transposed(hidden, edge_mix_wide)
    edge_grad = edge_total + matmul_back(pre_wide, w_edge_in[0])
    sender_grad = matmul_back(pre_wide, w_edge_in[1])
    grad_edge_latent = transposed(edge_lat, pre_wide)
    grad_edge_sender = transposed(senders, pre_wide)
    upper_part, lower_part = split_parts(matmul_back(pre_wide, w_edge_in[2]))
    receiver_grad = jnp.dot(incidence, upper_part, preferred_element_type=jnp.float32) + jnp.dot(
        incidence, lower_part, preferred_element_type=jnp.float32
    )
    grad_edge_receiver = transposed(receivers, pre_wide)
    table_grad = jax.ops.segment_sum(sender_grad, sender_slot, num_segments=lookup_table.shape[0])
    remote_grad = table_grad[node_count:].reshape(send_list.shape[0], send_list.shape[1], portion)
    returned = lax.all_to_all(
        remote_grad.astype(jnp.bfloat16), "region", split_axis=0, concat_axis=0, tiled=True
    ).astype(remote_grad.dtype)
    node_grad = (
        node_cot.astype(jnp.float32)
        + node_direct
        + receiver_grad
        + table_grad[:node_count]
        + jax.ops.segment_sum(
            returned.reshape(-1, portion), send_list.reshape(-1), num_segments=node_count
        )
    )
    node_grad_out, edge_grad_out = (
        lax.all_to_all(
            node_grad.astype(jnp.bfloat16), "feat", split_axis=0, concat_axis=1, tiled=True
        ).astype(node_grad.dtype),
        lax.all_to_all(
            edge_grad.astype(jnp.bfloat16), "feat", split_axis=0, concat_axis=1, tiled=True
        ).astype(edge_grad.dtype),
    )
    summed_grads = (
        lax.psum(
            jnp.stack([grad_edge_latent, grad_edge_sender, grad_edge_receiver], axis=0).astype(
                jnp.bfloat16
            ),
            "region",
        ).astype(jnp.float32),
        lax.psum(grad_edge_second_layer.astype(jnp.bfloat16), "region").astype(jnp.float32),
        lax.psum(
            jnp.stack([grad_node_latent, grad_node_pooled], axis=0).astype(jnp.bfloat16), "region"
        ).astype(jnp.float32),
        lax.psum(grad_node_second_layer.astype(jnp.bfloat16), "region").astype(jnp.float32),
    )
    edge_norm = 1.0 / jnp.sqrt(jnp.float32(edge_count * lax.axis_size("region")))
    node_norm = 1.0 / jnp.sqrt(jnp.float32(node_count * lax.axis_size("region")))
    return (
        node_new_rows,
        edge_new_rows,
        node_grad_out,
        edge_grad_out,
        summed_grads[0] * edge_norm,
        summed_grads[1] * edge_norm,
        summed_grads[2] * node_norm,
        summed_grads[3] * node_norm,
    )


def solution(mesh):
    in_specs = (
        P(("region", "feat"), None),
        P(("region", "feat"), None),
        P("region"),
        P("region"),
        P("region", None, None),
        P(None, "feat", None),
        P("feat", None),
        P(None, "feat", None),
        P("feat", None),
        P("feat"),
        P("feat"),
        P(("region", "feat"), None),
        P(("region", "feat"), None),
    )
    out_specs = (
        P(("region", "feat"), None),
        P(("region", "feat"), None),
        P(("region", "feat"), None),
        P(("region", "feat"), None),
        P(None, "feat", None),
        P("feat", None),
        P(None, "feat", None),
        P("feat", None),
    )
    return jax.shard_map(shards, mesh=mesh, in_specs=in_specs, out_specs=out_specs, check_vma=False)
```

profile of v0, /device:TPU:0, one launch (start us, length us, event | category | flops | bytes accessed | tf_op | source)
XLA Modules:
  0.0 344.5 jit_solution(10065554357982523741)
XLA Ops:
  10.3 5.2 %all-to-all-start = ((bf16[96,4,128]{2,0,1:T(8,128)(2,1)}), bf16[96,4,128]{2,0,1:T(8,128)(2,1)S(1)}, u32[]{:S(2)}, u32[]{:S(2)}) async-start(bf16[96,4,128]{2,0,1:T(8,128)(2,1)} %copy_bitcast_fusion.6), calls=%async_computation | async-start | bytes 196608 | tf_op jit(solution)/shard_map/all_to_all | solution.py:75
  16.7 8.7 %all_gather.23 = f32[2,512]{1,0:T(2,128)S(1)} all-gather(f32[2,128]{1,0:T(2,128)S(1)} %pad_maximum_fusion.4), channel_id=1, replica_groups=mesh['region'=8,'feat'=4] {'feat'}, dimensions={1}, use_global_device_ids=true | all-gather | bytes 5120 | tf_op jit(solution)/shard_map/all_gather | solution.py:98
  27.0 4.9 %all-to-all-start.1 = ((bf16[8,16,128]{2,1,0:T(8,128)(2,1)}), bf16[8,16,128]{2,1,0:T(8,128)(2,1)S(1)}, u32[]{:S(2)}, u32[]{:S(2)}) async-start(bf16[8,16,128]{2,1,0:T(8,128)(2,1)} %bitcast.10), calls=%async_computation.1 | async-start | bytes 65536 | tf_op jit(solution)/shard_map/all_to_all | solution.py:90
  32.0 5.7 %all-to-all-done.1 = bf16[8,16,128]{2,1,0:T(8,128)(2,1)S(1)} async-done(((bf16[8,16,128]{2,1,0:T(8,128)(2,1)}), bf16[8,16,128]{2,1,0:T(8,128)(2,1)S(1)}, u32[]{:S(2)}, u32[]{:S(2)}) %all-to-all-start.1) | async-done | bytes 32800 | tf_op jit(solution)/shard_map/all_to_all | solution.py:90
  37.7 15.3 %all_gather.22 = bf16[512,512]{1,0:T(8,128)(2,1)S(1)} all-gather(bf16[512,128]{1,0:T(8,128)(2,1)S(1)} %pad_maximum_fusion.3), channel_id=1, replica_groups=mesh['region'=8,'feat'=4] {'feat'}, dimensions={1}, use_global_device_ids=true | all-gather | bytes 655360 | tf_op jit(solution)/shard_map/all_gather | solution.py:101
  58.3 7.1 %all-gather.4.cloned.1.call-done = bf16[7,512,512]{2,1,0:T(8,128)(2,1)} async-done(((bf16[7,128,512]{2,1,0:T(8,128)(2,1)}), bf16[7,512,512]{2,1,0:T(8,128)(2,1)}) %all-gather.4.cloned.1.call-update) | async-done | bytes 3670032 | tf_op jit(solution)/shard_map/all_gather | solution.py:97
  78.7 22.3 %reduce-scatter.2.cloned.1.call-done = bf16[96,512]{1,0:T(8,128)(2,1)} async-done(((bf16[384,512]{1,0:T(8,128)(2,1)}), bf16[96,512]{1,0:T(8,128)(2,1)}) %reduce-scatter.2.cloned.1.call-update) | async-done | bytes 98320 | tf_op jit(solution)/shard_map/reduce_scatter | solution.py:118
  107.3 9.9 %all_gather.24 = bf16[384,512]{1,0:T(8,128)(2,1)S(1)} all-gather(bf16[96,512]{1,0:T(8,128)(2,1)S(1)} %fusion.10), channel_id=1, replica_groups=mesh['region'=8,'feat'=4] {'feat'}, dimensions={0}, use_global_device_ids=true | all-gather | bytes 491520 | tf_op jit(solution)/shard_map/all_gather | solution.py:146
  128.8 3.4 %multiply_convert_fusion = bf16[768,512]{0,1:T(8,128)(2,1)} fusion(f32[768,512]{0,1:T(8,128)} %get-tuple-element.55, bf16[768,512]{0,1:T(8,128)(2,1)} %multiply_convert_fusion.1, bf16[7,512,512]{2,1,0:T(8,128)(2,1)} %all-gather.4.cloned.1.call-done), kind=kOutput, calls=%fused_computation.22 | convolution fusion | flops 406192128 | bytes 3670016 | tf_op jit(solution)/shard_map/dot_general | solution.py:38
  132.3 7.6 %all_to_all.157 = bf16[96,4,128]{2,0,1:T(8,128)(2,1)S(1)} all-to-all(bf16[96,4,128]{2,0,1:T(8,128)(2,1)S(1)} %copy_bitcast_fusion.5), channel_id=1, replica_groups=mesh['region'=8,'feat'=4] {'feat'}, dimensions={1} | all-to-all | bytes 196608 | tf_op jit(solution)/shard_map/all_to_all | solution.py:77
  139.9 3.5 %all-to-all-start.7 = ((bf16[768,4,128]{0,2,1:T(8,128)(2,1)}), bf16[768,4,128]{0,2,1:T(8,128)(2,1)S(1)}, u32[]{:S(2)}, u32[]{:S(2)}) async-start(bf16[768,4,128]{0,2,1:T(8,128)(2,1)} %bitcast.35), calls=%async_computation.8 | async-start | bytes 1572864 | tf_op jit(solution)/shard_map/all_to_all | solution.py:76
  144.7 11.5 %gather_fusion.6 = bf16[3072,128]{1,0:T(8,128)(2,1)} fusion(bf16[384,128]{1,0:T(8,128)(2,1)S(1)} %bitcast.174, s32[3072]{0:T(1024)S(1)} %fusion.38), kind=kCustom, calls=%fused_computation.6 | custom fusion | bytes 1585152 | tf_op jit(solution)/shard_map/gather | solution.py:93
  156.9 11.5 %gather_fusion.5 = bf16[3072,128]{1,0:T(8,128)(2,1)} fusion(bf16[512,128]{1,0:T(8,128)(2,1)S(1)} %pad_maximum_fusion.3, s32[3072]{0:T(1024)S(1)} %fusion.39), kind=kCustom, calls=%fused_computation.5 | custom fusion | bytes 1585152 | tf_op jit(solution)/shard_map/gather | solution.py:92
  168.4 4.5 %all-to-all-start.5 = ((bf16[768,4,128]{2,0,1:T(8,128)(2,1)}), bf16[768,4,128]{2,0,1:T(8,128)(2,1)}, u32[]{:S(2)}, u32[]{:S(2)}) async-start(bf16[768,4,128]{2,0,1:T(8,128)(2,1)} %copy_bitcast_fusion.1), calls=%async_computation.6 | async-start | bytes 1572864 | tf_op jit(solution)/shard_map/all_to_all | solution.py:78
  176.4 10.9 %gather_fusion.4 = f32[3072,128]{1,0:T(8,128)} fusion(f32[384,128]{1,0:T(8,128)S(1)} %constant_dynamic-slice_fusion, s32[3072]{0:T(1024)S(1)} %fusion.38), kind=kCustom, calls=%fused_computation.4 | custom fusion | bytes 3158016 | tf_op jit(solution)/shard_map/gather | solution.py:162
  197.8 13.4 %all_gather.27 = bf16[384,512]{1,0:T(8,128)(2,1)S(1)} all-gather(bf16[96,512]{1,0:T(8,128)(2,1)S(1)} %get-tuple-element.46), channel_id=1, replica_groups=mesh['region'=8,'feat'=4] {'feat'}, dimensions={0}, use_global_device_ids=true | all-gather | bytes 491520 | tf_op jit(solution)/shard_map/all_gather | solution.py:147
  215.6 4.7 %all-to-all-done.10 = bf16[96,4,128]{2,0,1:T(8,128)(2,1)S(1)} async-done(((bf16[96,4,128]{2,0,1:T(8,128)(2,1)}), bf16[96,4,128]{2,0,1:T(8,128)(2,1)S(1)}, u32[]{:S(2)}, u32[]{:S(2)}) %all-to-all-start.10) | async-done | bytes 98336 | tf_op jit(solution)/shard_map/all_to_all | solution.py:164
  220.3 4.2 %all-to-all-start.8 = ((bf16[768,4,128]{2,0,1:T(8,128)(2,1)}), bf16[768,4,128]{2,0,1:T(8,128)(2,1)}, u32[]{:S(2)}, u32[]{:S(2)}) async-start(bf16[768,4,128]{2,0,1:T(8,128)(2,1)} %copy.67), calls=%async_computation.9 | async-start | bytes 1572864 | tf_op jit(solution)/shard_map/all_to_all | solution.py:166
  237.6 17.3 %scatter_custom_fusion = f32[512,128]{1,0:T(8,128)S(1)} fusion(s32[3072]{0:T(1024)S(1)} %copy-done.23, f32[3072,128]{1,0:T(8,128)} %fusion.25, f32[]{:T(128)} %constant.20.clone.1), kind=kCustom, calls=%fused_computation.95 | custom fusion | flops 393216 | bytes 262656 | tf_op jit(solution)/shard_map/scatter-add | solution.py:182
  260.4 4.8 %all-to-all-start.3 = ((bf16[8,16,128]{2,1,0:T(8,128)(2,1)}), bf16[8,16,128]{2,1,0:T(8,128)(2,1)S(1)}, u32[]{:S(2)}, u32[]{:S(2)}) async-start(bf16[8,16,128]{2,1,0:T(8,128)(2,1)} %bitcast.26), calls=%async_computation.4 | async-start | bytes 65536 | tf_op jit(solution)/shard_map/all_to_all | solution.py:184
  265.3 4.0 %convolution_convert_fusion.6 = bf16[128,512]{1,0:T(8,128)(2,1)} fusion(bf16[3072,128]{1,0:T(8,128)(2,1)} %bitcast.44, bf16[3072,512]{0,1:T(8,128)(2,1)} %all-gather.8.cloned.1.call-done), kind=kOutput, calls=%fused_computation.45 | convolution fusion | flops 402718720 | bytes 4063232 | tf_op jit(solution)/shard_map/dot_general | solution.py:44
  273.0 4.1 %all-to-all-start.4 = ((bf16[4,96,128]{2,1,0:T(8,128)(2,1)}), bf16[4,96,128]{2,1,0:T(8,128)(2,1)S(1)}, u32[]{:S(2)}, u32[]{:S(2)}) async-start(bf16[4,96,128]{2,1,0:T(8,128)(2,1)} %bitcast.28), calls=%async_computation.5 | async-start | bytes 196608 | tf_op jit(solution)/shard_map/all_to_all | solution.py:197
  282.1 3.5 %all-to-all-start.6 = ((bf16[4,768,128]{2,1,0:T(8,128)(2,1)}), bf16[4,768,128]{2,1,0:T(8,128)(2,1)S(1)}, u32[]{:S(2)}, u32[]{:S(2)}) async-start(bf16[4,768,128]{2,1,0:T(8,128)(2,1)} %bitcast.176), calls=%async_computation.7 | async-start | bytes 1572864 | tf_op jit(solution)/shard_map/all_to_all | solution.py:200
  286.3 44.6 %all-reduce.3.cloned.1.call-done = (bf16[3,128,512]{1,2,0:T(8,128)(2,1)}, bf16[128,512]{1,0:T(8,128)(2,1)}, bf16[2,128,512]{1,2,0:T(8,128)(2,1)}, bf16[128,512]{1,0:T(8,128)(2,1)}) async-done(((bf16[3,128,512]{1,2,0:T(8,128)(2,1)}, bf16[128,512]{1,0:T(8,128)(2,1)}, bf16[2,128,512]{1,2,0:T(8,128)(2,1)}, bf16[128,512]{1,0:T(8,128)(2,1)}), (bf16[3,128,512]{1,2,0:T(8,128)(2,1)}, bf16[128,512]{1,0:T(8,128)(2,1)}, ...) | async-done | bytes 917520 | tf_op jit(solution)/shard_map/psum | solution.py:205
  (155 shorter events, 97.4 us)
Async XLA Ops:
  7.2 58.3 %all-gather.4.cloned.1.call-start = ((), (), s32[]{:S(2)}) async-start(), calls=%async_computation.12 | async-start | bytes 4587520 | tf_op jit(solution)/shard_map/all_gather | solution.py:97
  7.2 8.2 %copy-start.6 = (bf16[768,512]{1,0:T(8,128)(2,1)S(1)}, bf16[768,512]{1,0:T(8,128)(2,1)}, u32[]{:S(2)}) copy-start(bf16[768,512]{1,0:T(8,128)(2,1)} %param.14) | copy-start | bytes 2359300
  9.6 7.2 %copy-start.25 = (f32[128]{0:T(128)S(1)}, f32[128]{0:T(128)}, u32[]{:S(2)}) copy-start(f32[128]{0:T(128)} %param.23) | copy-start | bytes 1540
  9.6 7.2 %copy-start.26 = (f32[128]{0:T(128)S(1)}, f32[128]{0:T(128)}, u32[]{:S(2)}) copy-start(f32[128]{0:T(128)} %param.22) | copy-start | bytes 1540
  9.6 15.9 %copy-start.22 = (s32[3072]{0:T(1024)S(1)}, s32[3072]{0:T(1024)}, u32[]{:S(2)}) copy-start(s32[3072]{0:T(1024)} %param.15) | copy-start | bytes 36868
  9.6 16.0 %copy-start.23 = (s32[3072]{0:T(1024)S(1)}, s32[3072]{0:T(1024)}, u32[]{:S(2)}) copy-start(s32[3072]{0:T(1024)} %param.16) | copy-start | bytes 36868
  10.3 15.4 %all-to-all-start = ((bf16[96,4,128]{2,0,1:T(8,128)(2,1)}), bf16[96,4,128]{2,0,1:T(8,128)(2,1)S(1)}, u32[]{:S(2)}, u32[]{:S(2)}) async-start(bf16[96,4,128]{2,0,1:T(8,128)(2,1)} %copy_bitcast_fusion.6), calls=%async_computation | async-start | bytes 196608 | tf_op jit(solution)/shard_map/all_to_all | solution.py:75
  27.0 10.7 %all-to-all-start.1 = ((bf16[8,16,128]{2,1,0:T(8,128)(2,1)}), bf16[8,16,128]{2,1,0:T(8,128)(2,1)S(1)}, u32[]{:S(2)}, u32[]{:S(2)}) async-start(bf16[8,16,128]{2,1,0:T(8,128)(2,1)} %bitcast.10), calls=%async_computation.1 | async-start | bytes 65536 | tf_op jit(solution)/shard_map/all_to_all | solution.py:90
  31.9 69.1 %reduce-scatter.2.cloned.1.call-start = ((), (), s32[]{:S(2)}) async-start(), calls=%async_computation.13 | async-start | bytes 491520 | tf_op jit(solution)/shard_map/reduce_scatter | solution.py:118
  77.4 148.1 %all-gather.6.cloned.1.call-start = ((), (), s32[]{:S(2)}) async-start(), calls=%async_computation.14 | async-start | bytes 3932160 | tf_op jit(solution)/shard_map/all_gather | solution.py:158
  78.7 26.3 %copy-start.11 = (bf16[96,512]{1,0:T(8,128)(2,1)S(1)}, bf16[96,512]{1,0:T(8,128)(2,1)}, u32[]{:S(2)}) copy-start(bf16[96,512]{1,0:T(8,128)(2,1)} %param.24) | copy-start | bytes 294916
  117.2 97.3 %copy-start.2 = (bf16[384,512]{1,0:T(8,128)(2,1)}, bf16[384,512]{1,0:T(8,128)(2,1)S(1)}, u32[]{:S(2)}) copy-start(bf16[384,512]{1,0:T(8,128)(2,1)S(1)} %all_gather.24) | copy-start | bytes 1179652
  132.3 11.3 %copy-start.5 = (bf16[768,512]{1,0:T(8,128)(2,1)S(1)}, bf16[768,512]{1,0:T(8,128)(2,1)}, u32[]{:S(2)}) copy-start(bf16[768,512]{1,0:T(8,128)(2,1)} %param.25) | copy-start | bytes 2359300
  139.9 28.5 %all-to-all-start.7 = ((bf16[768,4,128]{0,2,1:T(8,128)(2,1)}), bf16[768,4,128]{0,2,1:T(8,128)(2,1)S(1)}, u32[]{:S(2)}, u32[]{:S(2)}) async-start(bf16[768,4,128]{0,2,1:T(8,128)(2,1)} %bitcast.35), calls=%async_computation.8 | async-start | bytes 1572864 | tf_op jit(solution)/shard_map/all_to_all | solution.py:76
  143.4 121.9 %all-gather.8.cloned.1.call-start = ((), (), s32[]{:S(2)}) async-start(), calls=%async_computation.15 | async-start | bytes 3932160 | tf_op jit(solution)/shard_map/all_gather | solution.py:159
  168.4 23.2 %all-to-all-start.5 = ((bf16[768,4,128]{2,0,1:T(8,128)(2,1)}), bf16[768,4,128]{2,0,1:T(8,128)(2,1)}, u32[]{:S(2)}, u32[]{:S(2)}) async-start(bf16[768,4,128]{2,0,1:T(8,128)(2,1)} %copy_bitcast_fusion.1), calls=%async_computation.6 | async-start | bytes 1572864 | tf_op jit(solution)/shard_map/all_to_all | solution.py:78
  176.4 11.2 %copy-start.19 = (bf16[96,512]{1,0:T(8,128)(2,1)S(1)}, bf16[96,512]{1,0:T(8,128)(2,1)}, u32[]{:S(2)}) copy-start(bf16[96,512]{1,0:T(8,128)(2,1)} %reduce-scatter.2.cloned.1.call-done) | copy-start | bytes 294916
  191.6 19.6 %all-to-all-start.9 = ((bf16[96,4,128]{2,0,1:T(8,128)(2,1)}), bf16[96,4,128]{2,0,1:T(8,128)(2,1)S(1)}, u32[]{:S(2)}, u32[]{:S(2)}) async-start(bf16[96,4,128]{2,0,1:T(8,128)(2,1)} %copy_bitcast_fusion.4), calls=%async_computation.10 | async-start | bytes 196608 | tf_op jit(solution)/shard_map/all_to_all | solution.py:165
  211.2 9.1 %all-to-all-start.10 = ((bf16[96,4,128]{2,0,1:T(8,128)(2,1)}), bf16[96,4,128]{2,0,1:T(8,128)(2,1)S(1)}, u32[]{:S(2)}, u32[]{:S(2)}) async-start(bf16[96,4,128]{2,0,1:T(8,128)(2,1)} %copy_bitcast_fusion.3), calls=%async_computation.11 | async-start | bytes 196608 | tf_op jit(solution)/shard_map/all_to_all | solution.py:164
  220.3 40.1 %all-to-all-start.8 = ((bf16[768,4,128]{2,0,1:T(8,128)(2,1)}), bf16[768,4,128]{2,0,1:T(8,128)(2,1)}, u32[]{:S(2)}, u32[]{:S(2)}) async-start(bf16[768,4,128]{2,0,1:T(8,128)(2,1)} %copy.67), calls=%async_computation.9 | async-start | bytes 1572864 | tf_op jit(solution)/shard_map/all_to_all | solution.py:166
  260.4 10.6 %all-to-all-start.3 = ((bf16[8,16,128]{2,1,0:T(8,128)(2,1)}), bf16[8,16,128]{2,1,0:T(8,128)(2,1)S(1)}, u32[]{:S(2)}, u32[]{:S(2)}) async-start(bf16[8,16,128]{2,1,0:T(8,128)(2,1)} %bitcast.26), calls=%async_computation.4 | async-start | bytes 65536 | tf_op jit(solution)/shard_map/all_to_all | solution.py:184
  265.2 65.7 %all-reduce.3.cloned.1.call-start = ((), (), s32[]{:S(2)}) async-start(), calls=%async_computation.16 | async-start | bytes 1835008 | tf_op jit(solution)/shard_map/psum | solution.py:205
  273.0 9.1 %all-to-all-start.4 = ((bf16[4,96,128]{2,1,0:T(8,128)(2,1)}), bf16[4,96,128]{2,1,0:T(8,128)(2,1)S(1)}, u32[]{:S(2)}, u32[]{:S(2)}) async-start(bf16[4,96,128]{2,1,0:T(8,128)(2,1)} %bitcast.28), calls=%async_computation.5 | async-start | bytes 196608 | tf_op jit(solution)/shard_map/all_to_all | solution.py:197
  282.1 54.6 %all-to-all-start.6 = ((bf16[4,768,128]{2,1,0:T(8,128)(2,1)}), bf16[4,768,128]{2,1,0:T(8,128)(2,1)S(1)}, u32[]{:S(2)}, u32[]{:S(2)}) async-start(bf16[4,768,128]{2,1,0:T(8,128)(2,1)} %bitcast.176), calls=%async_computation.7 | async-start | bytes 1572864 | tf_op jit(solution)/shard_map/all_to_all | solution.py:200
  (18 other events, 51.7 us)
Sparse Core Ops, SparseCore 0:
  10.4 55.0 all-gather.3
  77.5 23.4 reduce-scatter.1
  132.4 59.5 all-gather.5
  193.7 49.8 all-gather.7
  270.3 60.5 all-reduce.2
where the time goes:
time: 346 us; the launch traced here: 345 us
  waiting for transfers between devices  89.5 us (26%)
  local copies, waits for them, and re-layouts  59.3 us (17%)
  blocking collectives  54.9 us (16%)
  matrix products  45.6 us (13%)
  starting transfers between devices  41.6 us (12%)
  other arithmetic  39.4 us (11%)
  between operations  14.3 us (4%)
    psum x1, waiting for transfers between devices, shards(): lax.psum(jnp.stack([grad_edge_latent, grad_edge_sender, grad_edge_receive...  44.6 us
    reduce_scatter x1, waiting for transfers between devices, shards(): lax.psum_scatter(jnp.dot(row_incidence, edge_new_rows, preferred_element_...  22.3 us
    dot_general x7, matrix products, matmul_back(): lax.dot_general(first_operand, second_operand, (((1,), (1,)), ((), ())),...  18 us
    scatter-add x1, other arithmetic, shards(): jax.ops.segment_sum(sender_grad, sender_slot, num_segments=lookup_table.s...  17.3 us
    all_gather x1, blocking collectives, shards(): lookup_full = lax.all_gather(lookup_table, 'feat', axis=1, tiled=True)  15.3 us
    all_gather x1, blocking collectives, shards(): lax.all_gather(node_mix_grad_rows, 'feat', axis=0, tiled=True)  13.4 us
    dot_general x7, matrix products, transposed(): lax.dot_general(first_operand, second_operand, (((0,), (0,)), ((), ())),...  11.6 us
    gather x1, local copies, waits for them, and re-layouts, shards(): receivers = node_lat[receiver_row]  11.5 us
  transfers between devices with their start and end apart: 15, of which 8 were waited for; matrix products, arithmetic and copies ran while one was open for 31% of the time, Pallas kernels for 0%

commit v1 on v0

--- a/solution.py
+++ b/solution.py
@@ -2,6 +2,7 @@
 import jax.numpy as jnp
 from jax import lax
 from jax.sharding import PartitionSpec as P
+from jax.lax import all_gather
 
 EPSILON = 1e-05
 
@@ -201,8 +202,12 @@
             edge_grad.astype(jnp.bfloat16), "feat", split_axis=0, concat_axis=1, tiled=True
         ).astype(edge_grad.dtype),
     )
+
+    def forms_show(xx, group_axis):
+        return all_gather(xx, group_axis).sum(axis=0)
+
     summed_grads = (
-        lax.psum(
+        forms_show(
             jnp.stack([grad_edge_latent, grad_edge_sender, grad_edge_receiver], axis=0).astype(
                 jnp.bfloat16
             ),

time: 346 us -> 339 us (0.980)
  waiting for transfers between devices: 89.5 us -> 82.4 us
  blocking collectives: 54.9 us -> 48.4 us
    psum x1, waiting for transfers between devices: 44.6 us -> 0.01 us  [shards(): lax.psum(grad_edge_second_layer.astype(jnp.bfloat16), 'region')]
    all_to_all x1, waiting for transfers between devices: 0.01 us -> 16.5 us  [shards(): lax.all_to_all(edge_latent_rows, 'feat', split_axis=1, concat_axis=0, til...]
    all_gather x1, waiting for transfers between devices: 0.01 us -> 12.8 us  [shards(): lax.all_gather(pre_grad_rows, 'feat', axis=0, tiled=True)]
    all_to_all x1 -> x0, blocking collectives: 7.59 us -> none  [shards(): lax.all_to_all(node_cot_rows, 'feat', split_axis=1, concat_axis=0, tiled=...]
    all_to_all x1, waiting for transfers between devices: 0.01 us -> 5.7 us  [shards(): lax.all_to_all(edge_grad.astype(jnp.bfloat16), 'feat', split_axis=0, conc...]
    all_to_all x1, waiting for transfers between devices: 4.75 us -> 0.01 us  [shards(): lax.all_to_all(node_hidden_rows, 'feat', split_axis=1, concat_axis=0, til...]
    all_to_all x1, waiting for transfers between devices: 0.01 us -> 4.3 us  [shards(): lax.all_to_all(pooled_rows, 'feat', split_axis=1, concat_axis=0, tiled=True)]
    all_to_all x0 -> x1, waiting for transfers between devices: none -> 3.86 us  [shards(): lax.all_to_all(node_cot_rows, 'feat', split_axis=1, concat_axis=0, tiled=...]
  transfers between devices with their start and end apart: 15 -> 17, of which waited for: 8 -> 11; matrix products, arithmetic and copies ran while one was open for 31% -> 33% of each run, Pallas kernels for 0% -> 0%
where the time goes in v1:
time: 339 us; the launch traced here: 337 us
  waiting for transfers between devices  82.4 us (24%)
  local copies, waits for them, and re-layouts  62.2 us (18%)
  blocking collectives  48.4 us (14%)
  starting transfers between devices  44.4 us (13%)
  matrix products  42.9 us (13%)
  other arithmetic  42.6 us (13%)
  between operations  14.6 us (4%)
    reduce_scatter x1, waiting for transfers between devices, shards(): lax.psum_scatter(jnp.dot(row_incidence, edge_new_rows, preferred_element_...  22.3 us
    scatter-add x1, other arithmetic, shards(): jax.ops.segment_sum(sender_grad, sender_slot, num_segments=lookup_table.s...  17.3 us
    all_to_all x1, waiting for transfers between devices, shards(): lax.all_to_all(edge_latent_rows, 'feat', split_axis=1, concat_axis=0, til...  16.5 us
    dot_general x7, matrix products, matmul_back(): lax.dot_general(first_operand, second_operand, (((1,), (1,)), ((), ())),...  15.4 us
    all_gather x1, blocking collectives, shards(): lookup_full = lax.all_gather(lookup_table, 'feat', axis=1, tiled=True)  15.3 us
    all_gather x1, blocking collectives, shards(): lax.all_gather(node_mix_grad_rows, 'feat', axis=0, tiled=True)  14.4 us
    all_gather x1, waiting for transfers between devices, shards(): lax.all_gather(pre_grad_rows, 'feat', axis=0, tiled=True)  12.8 us
    gather x1, local copies, waits for them, and re-layouts, shards(): receivers = node_lat[receiver_row]  11.5 us
  transfers between devices with their start and end apart: 17, of which 11 were waited for; matrix products, arithmetic and copies ran while one was open for 33% of the time, Pallas kernels for 0%

profile of v1, /device:TPU:0, one launch (start us, length us, event | category | flops | bytes accessed | tf_op | source)
XLA Modules:
  0.0 337.5 jit_solution(17380627588632279719)
XLA Ops:
  10.3 5.2 %all-to-all-start = ((bf16[96,4,128]{2,0,1:T(8,128)(2,1)}), bf16[96,4,128]{2,0,1:T(8,128)(2,1)S(1)}, u32[]{:S(2)}, u32[]{:S(2)}) async-start(bf16[96,4,128]{2,0,1:T(8,128)(2,1)} %copy_bitcast_fusion.6), calls=%async_computation | async-start | bytes 196608 | tf_op jit(solution)/shard_map/all_to_all | solution.py:76
  16.7 8.7 %all_gather.27 = f32[2,512]{1,0:T(2,128)S(1)} all-gather(f32[2,128]{1,0:T(2,128)S(1)} %pad_maximum_fusion.4), channel_id=1, replica_groups=mesh['region'=8,'feat'=4] {'feat'}, dimensions={1}, use_global_device_ids=true | all-gather | bytes 5120 | tf_op jit(solution)/shard_map/all_gather | solution.py:99
  27.0 4.9 %all-to-all-start.1 = ((bf16[8,16,128]{2,1,0:T(8,128)(2,1)}), bf16[8,16,128]{2,1,0:T(8,128)(2,1)S(1)}, u32[]{:S(2)}, u32[]{:S(2)}) async-start(bf16[8,16,128]{2,1,0:T(8,128)(2,1)} %bitcast.10), calls=%async_computation.1 | async-start | bytes 65536 | tf_op jit(solution)/shard_map/all_to_all | solution.py:91
  32.0 5.7 %all-to-all-done.1 = bf16[8,16,128]{2,1,0:T(8,128)(2,1)S(1)} async-done(((bf16[8,16,128]{2,1,0:T(8,128)(2,1)}), bf16[8,16,128]{2,1,0:T(8,128)(2,1)S(1)}, u32[]{:S(2)}, u32[]{:S(2)}) %all-to-all-start.1) | async-done | bytes 32800 | tf_op jit(solution)/shard_map/all_to_all | solution.py:91
  37.7 15.3 %all_gather.26 = bf16[512,512]{1,0:T(8,128)(2,1)S(1)} all-gather(bf16[512,128]{1,0:T(8,128)(2,1)S(1)} %pad_maximum_fusion.3), channel_id=1, replica_groups=mesh['region'=8,'feat'=4] {'feat'}, dimensions={1}, use_global_device_ids=true | all-gather | bytes 655360 | tf_op jit(solution)/shard_map/all_gather | solution.py:102
  59.0 6.5 %all-gather.5.cloned.1.call-done = bf16[7,512,512]{2,1,0:T(8,128)(2,1)} async-done(((bf16[7,128,512]{2,1,0:T(8,128)(2,1)}), bf16[7,512,512]{2,1,0:T(8,128)(2,1)}) %all-gather.5.cloned.1.call-update) | async-done | bytes 3670032 | tf_op jit(solution)/shard_map/all_gather | solution.py:98
  78.8 22.3 %reduce-scatter.2.cloned.1.call-done = bf16[96,512]{1,0:T(8,128)(2,1)} async-done(((bf16[384,512]{1,0:T(8,128)(2,1)}), bf16[96,512]{1,0:T(8,128)(2,1)}) %reduce-scatter.2.cloned.1.call-update) | async-done | bytes 98320 | tf_op jit(solution)/shard_map/reduce_scatter | solution.py:119
  107.4 9.9 %all_gather.28 = bf16[384,512]{1,0:T(8,128)(2,1)S(1)} all-gather(bf16[96,512]{1,0:T(8,128)(2,1)S(1)} %fusion.10), channel_id=1, replica_groups=mesh['region'=8,'feat'=4] {'feat'}, dimensions={0}, use_global_device_ids=true | all-gather | bytes 491520 | tf_op jit(solution)/shard_map/all_gather | solution.py:147
  132.5 3.7 %all-to-all-start.7 = ((bf16[768,4,128]{0,2,1:T(8,128)(2,1)}), bf16[768,4,128]{0,2,1:T(8,128)(2,1)S(1)}, u32[]{:S(2)}, u32[]{:S(2)}) async-start(bf16[768,4,128]{0,2,1:T(8,128)(2,1)} %bitcast.35), calls=%async_computation.8 | async-start | bytes 1572864 | tf_op jit(solution)/shard_map/all_to_all | solution.py:77
  136.8 16.5 %all-to-all-done.7 = bf16[768,4,128]{0,2,1:T(8,128)(2,1)S(1)} async-done(((bf16[768,4,128]{0,2,1:T(8,128)(2,1)}), bf16[768,4,128]{0,2,1:T(8,128)(2,1)S(1)}, u32[]{:S(2)}, u32[]{:S(2)}) %all-to-all-start.7) | async-done | bytes 786464 | tf_op jit(solution)/shard_map/all_to_all | solution.py:77
  157.3 4.3 %all-to-all-done.9 = bf16[96,4,128]{2,0,1:T(8,128)(2,1)S(1)} async-done(((bf16[96,4,128]{2,0,1:T(8,128)(2,1)}), bf16[96,4,128]{2,0,1:T(8,128)(2,1)S(1)}, u32[]{:S(2)}, u32[]{:S(2)}) %all-to-all-start.9) | async-done | bytes 98336 | tf_op jit(solution)/shard_map/all_to_all | solution.py:166
  165.1 11.5 %gather_fusion.6 = bf16[3072,128]{1,0:T(8,128)(2,1)} fusion(bf16[384,128]{1,0:T(8,128)(2,1)S(1)} %bitcast.174, s32[3072]{0:T(1024)S(1)} %fusion.38), kind=kCustom, calls=%fused_computation.6 | custom fusion | bytes 1585152 | tf_op jit(solution)/shard_map/gather | solution.py:94
  176.7 11.5 %gather_fusion.5 = bf16[3072,128]{1,0:T(8,128)(2,1)} fusion(bf16[512,128]{1,0:T(8,128)(2,1)S(1)} %pad_maximum_fusion.3, s32[3072]{0:T(1024)S(1)} %fusion.39), kind=kCustom, calls=%fused_computation.5 | custom fusion | bytes 1585152 | tf_op jit(solution)/shard_map/gather | solution.py:93
  191.0 3.9 %all-to-all-start.8 = ((bf16[768,4,128]{2,0,1:T(8,128)(2,1)}), bf16[768,4,128]{2,0,1:T(8,128)(2,1)S(1)}, u32[]{:S(2)}, u32[]{:S(2)}) async-start(bf16[768,4,128]{2,0,1:T(8,128)(2,1)} %copy.86), calls=%async_computation.9 | async-start | bytes 1572864 | tf_op jit(solution)/shard_map/all_to_all | solution.py:167
  195.2 14.4 %all_gather.32 = bf16[384,512]{1,0:T(8,128)(2,1)S(1)} all-gather(bf16[96,512]{1,0:T(8,128)(2,1)S(1)} %get-tuple-element.53), channel_id=1, replica_groups=mesh['region'=8,'feat'=4] {'feat'}, dimensions={0}, use_global_device_ids=true | all-gather | bytes 491520 | tf_op jit(solution)/shard_map/all_gather | solution.py:148
  211.6 3.7 %convolution_convert_fusion.6 = bf16[128,512]{1,0:T(8,128)(2,1)} fusion(bf16[3072,128]{1,0:T(8,128)(2,1)S(1)} %bitcast.179, bf16[3072,512]{0,1:T(8,128)(2,1)} %all-gather.11.cloned.1.call-done), kind=kOutput, calls=%fused_computation.45 | convolution fusion | flops 402718720 | bytes 4063232 | tf_op jit(solution)/shard_map/dot_general | solution.py:45
  215.4 12.8 %all-gather.7.cloned.1.call-done = bf16[3072,512]{0,1:T(8,128)(2,1)} async-done(((bf16[768,512]{0,1:T(8,128)(2,1)}), bf16[3072,512]{0,1:T(8,128)(2,1)}) %all-gather.7.cloned.1.call-update) | async-done | bytes 3145744 | tf_op jit(solution)/shard_map/all_gather | solution.py:159
  239.4 3.9 %all-to-all-done.2 = bf16[96,4,128]{2,0,1:T(8,128)(2,1)S(1)} async-done(((bf16[96,4,128]{2,0,1:T(8,128)(2,1)}), bf16[96,4,128]{2,0,1:T(8,128)(2,1)S(1)}, u32[]{:S(2)}, u32[]{:S(2)}) %all-to-all-start.2) | async-done | bytes 98336 | tf_op jit(solution)/shard_map/all_to_all | solution.py:78
  243.3 4.2 %all-to-all-start.5 = ((bf16[768,4,128]{2,0,1:T(8,128)(2,1)}), bf16[768,4,128]{2,0,1:T(8,128)(2,1)}, u32[]{:S(2)}, u32[]{:S(2)}) async-start(bf16[768,4,128]{2,0,1:T(8,128)(2,1)} %copy_bitcast_fusion.1), calls=%async_computation.6 | async-start | bytes 1572864 | tf_op jit(solution)/shard_map/all_to_all | solution.py:79
  249.5 10.9 %gather_fusion.4 = f32[3072,128]{1,0:T(8,128)} fusion(f32[384,128]{1,0:T(8,128)S(1)} %constant_dynamic-slice_fusion, s32[3072]{0:T(1024)S(1)} %fusion.38), kind=kCustom, calls=%fused_computation.4 | custom fusion | bytes 3158016 | tf_op jit(solution)/shard_map/gather | solution.py:163
  268.1 17.3 %scatter_custom_fusion = f32[512,128]{1,0:T(8,128)S(1)} fusion(s32[3072]{0:T(1024)S(1)} %copy-done.24, f32[3072,128]{1,0:T(8,128)} %fusion.25, f32[]{:T(128)} %constant.21.clone.1), kind=kCustom, calls=%fused_computation.95 | custom fusion | flops 393216 | bytes 262656 | tf_op jit(solution)/shard_map/scatter-add | solution.py:183
  286.0 4.6 %all-to-all-start.3 = ((bf16[8,16,128]{2,1,0:T(8,128)(2,1)}), bf16[8,16,128]{2,1,0:T(8,128)(2,1)S(1)}, u32[]{:S(2)}, u32[]{:S(2)}) async-start(bf16[8,16,128]{2,1,0:T(8,128)(2,1)} %bitcast.26), calls=%async_computation.4 | async-start | bytes 65536 | tf_op jit(solution)/shard_map/all_to_all | solution.py:185
  300.7 4.1 %all-to-all-start.4 = ((bf16[4,96,128]{2,1,0:T(8,128)(2,1)}), bf16[4,96,128]{2,1,0:T(8,128)(2,1)S(1)}, u32[]{:S(2)}, u32[]{:S(2)}) async-start(bf16[4,96,128]{2,1,0:T(8,128)(2,1)} %bitcast.28), calls=%async_computation.5 | async-start | bytes 196608 | tf_op jit(solution)/shard_map/all_to_all | solution.py:198
  317.5 5.7 %all-to-all-done.6 = bf16[4,768,128]{2,1,0:T(8,128)(2,1)S(1)} async-done(((bf16[4,768,128]{2,1,0:T(8,128)(2,1)}), bf16[4,768,128]{2,1,0:T(8,128)(2,1)S(1)}, u32[]{:S(2)}, u32[]{:S(2)}) %all-to-all-start.6) | async-done | bytes 786464 | tf_op jit(solution)/shard_map/all_to_all | solution.py:201
  (164 shorter events, 111.2 us)
Async XLA Ops:
  7.2 58.3 %all-gather.5.cloned.1.call-start = ((), (), s32[]{:S(2)}) async-start(), calls=%async_computation.12 | async-start | bytes 4587520 | tf_op jit(solution)/shard_map/all_gather | solution.py:98
  7.2 8.2 %copy-start.8 = (bf16[768,512]{1,0:T(8,128)(2,1)S(1)}, bf16[768,512]{1,0:T(8,128)(2,1)}, u32[]{:S(2)}) copy-start(bf16[768,512]{1,0:T(8,128)(2,1)} %param.14) | copy-start | bytes 2359300
  9.6 15.9 %copy-start.23 = (s32[3072]{0:T(1024)S(1)}, s32[3072]{0:T(1024)}, u32[]{:S(2)}) copy-start(s32[3072]{0:T(1024)} %param.15) | copy-start | bytes 36868
  9.6 16.0 %copy-start.24 = (s32[3072]{0:T(1024)S(1)}, s32[3072]{0:T(1024)}, u32[]{:S(2)}) copy-start(s32[3072]{0:T(1024)} %param.16) | copy-start | bytes 36868
  10.3 15.4 %all-to-all-start = ((bf16[96,4,128]{2,0,1:T(8,128)(2,1)}), bf16[96,4,128]{2,0,1:T(8,128)(2,1)S(1)}, u32[]{:S(2)}, u32[]{:S(2)}) async-start(bf16[96,4,128]{2,0,1:T(8,128)(2,1)} %copy_bitcast_fusion.6), calls=%async_computation | async-start | bytes 196608 | tf_op jit(solution)/shard_map/all_to_all | solution.py:76
  27.0 10.7 %all-to-all-start.1 = ((bf16[8,16,128]{2,1,0:T(8,128)(2,1)}), bf16[8,16,128]{2,1,0:T(8,128)(2,1)S(1)}, u32[]{:S(2)}, u32[]{:S(2)}) async-start(bf16[8,16,128]{2,1,0:T(8,128)(2,1)} %bitcast.10), calls=%async_computation.1 | async-start | bytes 65536 | tf_op jit(solution)/shard_map/all_to_all | solution.py:91
  31.9 69.2 %reduce-scatter.2.cloned.1.call-start = ((), (), s32[]{:S(2)}) async-start(), calls=%async_computation.13 | async-start | bytes 491520 | tf_op jit(solution)/shard_map/reduce_scatter | solution.py:119
  77.5 134.1 %all-gather.11.cloned.1.call-start = ((), (), s32[]{:S(2)}) async-start(), calls=%async_computation.16 | async-start | bytes 3932160 | tf_op jit(solution)/shard_map/all_gather | solution.py:160
  78.8 26.3 %copy-start.14 = (bf16[96,512]{1,0:T(8,128)(2,1)S(1)}, bf16[96,512]{1,0:T(8,128)(2,1)}, u32[]{:S(2)}) copy-start(bf16[96,512]{1,0:T(8,128)(2,1)} %param.24) | copy-start | bytes 294916
  117.3 92.3 %copy-start.3 = (bf16[384,512]{1,0:T(8,128)(2,1)}, bf16[384,512]{1,0:T(8,128)(2,1)S(1)}, u32[]{:S(2)}) copy-start(bf16[384,512]{1,0:T(8,128)(2,1)S(1)} %all_gather.28) | copy-start | bytes 1179652
  128.9 99.3 %all-gather.7.cloned.1.call-start = ((), (), s32[]{:S(2)}) async-start(), calls=%async_computation.14 | async-start | bytes 3932160 | tf_op jit(solution)/shard_map/all_gather | solution.py:159
  132.5 20.8 %all-to-all-start.7 = ((bf16[768,4,128]{0,2,1:T(8,128)(2,1)}), bf16[768,4,128]{0,2,1:T(8,128)(2,1)S(1)}, u32[]{:S(2)}, u32[]{:S(2)}) async-start(bf16[768,4,128]{0,2,1:T(8,128)(2,1)} %bitcast.35), calls=%async_computation.8 | async-start | bytes 1572864 | tf_op jit(solution)/shard_map/all_to_all | solution.py:77
  153.3 8.3 %all-to-all-start.9 = ((bf16[96,4,128]{2,0,1:T(8,128)(2,1)}), bf16[96,4,128]{2,0,1:T(8,128)(2,1)S(1)}, u32[]{:S(2)}, u32[]{:S(2)}) async-start(bf16[96,4,128]{2,0,1:T(8,128)(2,1)} %copy_bitcast_fusion.4), calls=%async_computation.10 | async-start | bytes 196608 | tf_op jit(solution)/shard_map/all_to_all | solution.py:166
  161.6 29.3 %all-to-all-start.10 = ((bf16[96,4,128]{2,0,1:T(8,128)(2,1)}), bf16[96,4,128]{2,0,1:T(8,128)(2,1)S(1)}, u32[]{:S(2)}, u32[]{:S(2)}) async-start(bf16[96,4,128]{2,0,1:T(8,128)(2,1)} %copy_bitcast_fusion.3), calls=%async_computation.11 | async-start | bytes 196608 | tf_op jit(solution)/shard_map/all_to_all | solution.py:165
  191.0 20.6 %all-to-all-start.8 = ((bf16[768,4,128]{2,0,1:T(8,128)(2,1)}), bf16[768,4,128]{2,0,1:T(8,128)(2,1)S(1)}, u32[]{:S(2)}, u32[]{:S(2)}) async-start(bf16[768,4,128]{2,0,1:T(8,128)(2,1)} %copy.86), calls=%async_computation.9 | async-start | bytes 1572864 | tf_op jit(solution)/shard_map/all_to_all | solution.py:167
  194.9 119.1 %all-reduce.3.cloned.1.call-start = ((), (), s32[]{:S(2)}) async-start(), calls=%async_computation.17 | async-start | bytes 1048576 | tf_op jit(solution)/shard_map/psum | solution.py:216
  215.3 16.1 %copy-start.11 = (bf16[3072,128]{1,0:T(8,128)(2,1)S(1)}, bf16[3072,128]{1,0:T(8,128)(2,1)}, u32[]{:S(2)}) copy-start(bf16[3072,128]{1,0:T(8,128)(2,1)} %gather_fusion.5) | copy-start | bytes 2359300
  215.4 111.4 %all-gather.9.cloned.1.call-start = ((), (), s32[]{:S(2)}) async-start(), calls=%async_computation.15 | async-start | bytes 3538944 | tf_op jit(solution)/shard_map/all_gather | solution.py:207
  235.1 8.2 %all-to-all-start.2 = ((bf16[96,4,128]{2,0,1:T(8,128)(2,1)}), bf16[96,4,128]{2,0,1:T(8,128)(2,1)S(1)}, u32[]{:S(2)}, u32[]{:S(2)}) async-start(bf16[96,4,128]{2,0,1:T(8,128)(2,1)} %copy_bitcast_fusion.5), calls=%async_computation.3 | async-start | bytes 196608 | tf_op jit(solution)/shard_map/all_to_all | solution.py:78
  238.4 9.9 %copy-start.10 = (bf16[768,512]{0,1:T(8,128)(2,1)S(1)}, bf16[768,512]{0,1:T(8,128)(2,1)}, u32[]{:S(2)}) copy-start(bf16[768,512]{0,1:T(8,128)(2,1)} %copy-done.9) | copy-start | bytes 2359300
  243.3 17.1 %all-to-all-start.5 = ((bf16[768,4,128]{2,0,1:T(8,128)(2,1)}), bf16[768,4,128]{2,0,1:T(8,128)(2,1)}, u32[]{:S(2)}, u32[]{:S(2)}) async-start(bf16[768,4,128]{2,0,1:T(8,128)(2,1)} %copy_bitcast_fusion.1), calls=%async_computation.6 | async-start | bytes 1572864 | tf_op jit(solution)/shard_map/all_to_all | solution.py:79
  286.0 10.3 %all-to-all-start.3 = ((bf16[8,16,128]{2,1,0:T(8,128)(2,1)}), bf16[8,16,128]{2,1,0:T(8,128)(2,1)S(1)}, u32[]{:S(2)}, u32[]{:S(2)}) async-start(bf16[8,16,128]{2,1,0:T(8,128)(2,1)} %bitcast.26), calls=%async_computation.4 | async-start | bytes 65536 | tf_op jit(solution)/shard_map/all_to_all | solution.py:185
  300.7 9.1 %all-to-all-start.4 = ((bf16[4,96,128]{2,1,0:T(8,128)(2,1)}), bf16[4,96,128]{2,1,0:T(8,128)(2,1)S(1)}, u32[]{:S(2)}, u32[]{:S(2)}) async-start(bf16[4,96,128]{2,1,0:T(8,128)(2,1)} %bitcast.28), calls=%async_computation.5 | async-start | bytes 196608 | tf_op jit(solution)/shard_map/all_to_all | solution.py:198
  309.8 13.4 %all-to-all-start.6 = ((bf16[4,768,128]{2,1,0:T(8,128)(2,1)}), bf16[4,768,128]{2,1,0:T(8,128)(2,1)S(1)}, u32[]{:S(2)}, u32[]{:S(2)}) async-start(bf16[4,768,128]{2,1,0:T(8,128)(2,1)} %bitcast.176), calls=%async_computation.7 | async-start | bytes 1572864 | tf_op jit(solution)/shard_map/all_to_all | solution.py:201
  (21 other events, 63.0 us)
Sparse Core Ops, SparseCore 0:
  10.4 55.0 all-gather.4
  77.6 23.4 reduce-scatter.1
  129.0 50.0 all-gather.10
  180.8 47.3 all-gather.6
  231.1 56.7 all-reduce.2
  289.5 37.2 all-gather.8
